TPU v7x, 16 devices: a whole 2x2x2 slice. The times are simulated.
16 devices in a mesh: dp: 2 (over z), pp: 8 (over y, x, core).
Axes of the slice: x: 2, y: 2, z: 2, core: 2. Of those that a mesh axis runs over, the one named last changes fastest.
Arguments:
- x: bfloat16 [8, 1024, 768], P(None, 'dp')
- t: bfloat16 [8, 1024, 768], P(None, 'dp')
- w1: bfloat16 [8, 2, 768, 3072], P('pp')
- w2: bfloat16 [8, 2, 3072, 768], P('pp')
Outputs:
- output 1: float32 [8, 2, 768, 3072], P('pp')
- output 2: float32 [8, 2, 3072, 768], P('pp')
- output 3: float32 [], replicated
All inputs are finite; a program needn't handle non-finite values.
Results may differ from a plain program's by a relative error of at most 0.00419436.
Values are sent between devices in bfloat16 or wider.
A program may use at most 1 GiB of HBM per device.

v0:
```python
import math
import jax
import jax.numpy as jnp
from jax import lax
from jax.sharding import PartitionSpec as P


def _gelu(u):
    c = math.sqrt(2.0 / math.pi)
    return 0.5 * u * (1.0 + jnp.tanh(c * (u + 0.044715 * u * u * u)))


def _dgelu(u):
    c = math.sqrt(2.0 / math.pi)
    th = jnp.tanh(c * (u + 0.044715 * u * u * u))
    return 0.5 * (1.0 + th) + 0.5 * u * (1.0 - th * th) * c * (1.0 + 3.0 * 0.044715 * u * u)


def solution(mesh):
    ndp = mesh.shape['dp']
    npp = mesh.shape['pp']
    down = [(i, i + 1) for i in range(npp - 1)]
    up = [(i + 1, i) for i in range(npp - 1)]

    def body(x, t, w1, w2):
        nm, tok, d = x.shape
        ff = w1.shape[-1]
        w1 = w1[0]
        w2 = w2[0]
        s = lax.axis_index('pp')
        first = s == 0
        last = s == npp - 1
        inv = 1.0 / (nm * tok * ndp * d)
        nsteps = nm + npp - 1

        def fwd_step(k, c):
            recv, hbuf, ubuf, dybuf, lsum = c
            m = k - s
            valid = (m >= 0) & (m < nm)
            mc = jnp.clip(m, 0, nm - 1)
            h = jnp.where(first, x[mc], recv)
            for j in range(2):
                u = jnp.dot(h, w1[j], preferred_element_type=jnp.float32).astype(jnp.bfloat16)
                a = _gelu(u.astype(jnp.float32)).astype(jnp.bfloat16)
                hbuf = hbuf.at[j, mc].set(jnp.where(valid, h, hbuf[j, mc]))
                ubuf = ubuf.at[j, mc].set(jnp.where(valid, u, ubuf[j, mc]))
                h = (h.astype(jnp.float32) + jnp.dot(a, w2[j], preferred_element_type=jnp.float32)).astype(jnp.bfloat16)
            r = h.astype(jnp.float32) - t[mc].astype(jnp.float32)
            keep = valid & last
            lsum = lsum + jnp.where(keep, 0.5 * jnp.sum(r * r), 0.0)
            dybuf = dybuf.at[mc].set(jnp.where(keep, (r * inv).astype(jnp.bfloat16), dybuf[mc]))
            recv = lax.ppermute(h, 'pp', down)
            return recv, hbuf, ubuf, dybuf, lsum

        init = (jnp.zeros((tok, d), jnp.bfloat16),
                jnp.zeros((2, nm, tok, d), jnp.bfloat16),
                jnp.zeros((2, nm, tok, ff), jnp.bfloat16),
                jnp.zeros((nm, tok, d), jnp.bfloat16),
                jnp.zeros((), jnp.float32))
        _, hbuf, ubuf, dybuf, lsum = lax.fori_loop(0, nsteps, fwd_step, init)

        def bwd_step(k, c):
            recv, dw1, dw2 = c
            m = k - (npp - 1 - s)
            valid = (m >= 0) & (m < nm)
            mc = jnp.clip(m, 0, nm - 1)
            g = jnp.where(last, dybuf[mc], recv)
            g = jnp.where(valid, g, jnp.zeros_like(g))
            for j in (1, 0):
                h = hbuf[j, mc]
                uf = ubuf[j, mc].astype(jnp.float32)
                a = _gelu(uf).astype(jnp.bfloat16)
                q = jnp.dot(g, w2[j].T, preferred_element_type=jnp.float32)
                e = (_dgelu(uf) * q).astype(jnp.bfloat16)
                dw2 = dw2.at[j].add(jnp.dot(a.T, g, preferred_element_type=jnp.float32))
                dw1 = dw1.at[j].add(jnp.dot(h.T, e, preferred_element_type=jnp.float32))
                g = (g.astype(jnp.float32) + jnp.dot(e, w1[j].T, preferred_element_type=jnp.float32)).astype(jnp.bfloat16)
            recv = lax.ppermute(g, 'pp', up)
            return recv, dw1, dw2

        init = (jnp.zeros((tok, d), jnp.bfloat16),
                jnp.zeros((2, d, ff), jnp.float32),
                jnp.zeros((2, ff, d), jnp.float32))
        _, dw1, dw2 = lax.fori_loop(0, nsteps, bwd_step, init)
        dw1 = lax.psum(dw1, 'dp')
        dw2 = lax.psum(dw2, 'dp')
        loss = lax.psum(lsum * inv, ('dp', 'pp'))
        return dw1[None], dw2[None], loss

    return jax.shard_map(body, mesh=mesh,
                         in_specs=(P(None, 'dp', None), P(None, 'dp', None), P('pp'), P('pp')),
                         out_specs=(P('pp'), P('pp'), P()), check_vma=False)
```

profile of v0, /device:TPU:0, one launch (start us, length us, event | category | flops | bytes accessed | tf_op | source)
XLA Modules:
  0.0 2924.6 jit_solution(13803682204513646297)
XLA Ops:
  7.2 16.3 broadcast_in_dim.33
  32.3 939.5 %while.49 = (s32[]{:T(128)}, bf16[512,768]{1,0:T(8,128)(2,1)S(1)}, bf16[2,8,512,768]{3,2,1,0:T(8,128)(2,1)}, bf16[2,8,512,3072]{3,2,1,0:T(8,128)(2,1)}, bf16[8,5...) while((s32[]{:T(128)}, bf16[512,768]{1,0:T(8,128)(2,1)S(1)}, ...), condition=%wide.region_5.6_spmd, body=%wide.region_0.5_spmd.sunk | while | flops 9713614848 | bytes 113252384 | solution.py:60
  990.0 1039.4 %while.50 = (s32[]{:T(128)}, bf16[512,768]{1,0:T(8,128)(2,1)}, f32[2,768,3072]{2,1,0:T(8,128)}, f32[2,3072,768]{2,1,0:T(8,128)}, s32[]{:T(128)}, /*index=5*/pred...) while((s32[]{:T(128)}, bf16[512,768]{1,0:T(8,128)(2,1)}, ...), condition=%wide.region_7.8_spmd, body=%wide.region_6.7_spmd.sunk | while | flops 19434307584 | bytes 208404912 | solution.py:84
  1041.1 12.2 fusion.202
  1109.4 12.2 fusion.202
  1177.7 12.2 fusion.202
  1245.9 12.2 fusion.202
  1314.2 12.2 fusion.202
  1382.5 12.2 fusion.202
  1450.7 12.2 fusion.202
  1519.0 12.2 fusion.202
  1575.2 12.3 fusion.201
  1587.5 12.3 fusion.202
  1643.8 12.3 fusion.201
  1656.1 12.3 fusion.202
  1724.5 12.2 fusion.202
  1780.6 12.3 fusion.201
  1792.9 12.3 fusion.202
  1917.5 12.4 fusion.201
  1929.8 12.3 fusion.202
  1998.2 12.2 fusion.202
  2029.4 69.2 %psum.23 = f32[]{:T(128)} all-reduce(f32[]{:T(128)S(6)} %mul.398), channel_id=1, replica_groups=mesh['dp'=2,'pp'=8] {'dp','pp'}, use_global_device_ids=true, to_apply=%region_10.11 | all-reduce | flops 1 | bytes 8 | tf_op jit(solution)/shard_map/psum | solution.py:87
  2098.7 793.5 %all-reduce.3.cloned.1.call-done = (f32[1,2,768,3072]{3,2,1,0:T(8,128)}, f32[1,2,3072,768]{3,2,1,0:T(8,128)}) async-done(((f32[1,2,768,3072]{3,2,1,0:T(8,128)}, f32[1,2,3072,768]{3,2,1,0:T(8,128)}), (f32[1,2,768,3072]{3,2,1,0:T(8,128)}, f32[1,2,3072,768]{3,2,1,0:T(8,128)})) %all-reduce.3.cloned.1.call-update) | async-done | bytes 37748752 | tf_op jit(solution)/shard_map/psum | solution.py:85
  2892.2 14.0 copy.48
  (792 shorter events, 1769.2 us)
Async XLA Ops:
  7.2 2885.0 %all-reduce.3.cloned.1.call-start = ((), (), s32[]{:S(2)}) async-start(), calls=%async_computation | async-start | bytes 75497472 | tf_op jit(solution)/shard_map/psum | solution.py:85
  200.7 13.3 collective-permute-start
  326.8 13.4 collective-permute-start
  516.2 13.4 collective-permute-start
  642.3 13.4 collective-permute-start
  705.5 13.3 collective-permute-start
  768.6 13.3 collective-permute-start
  894.6 13.3 collective-permute-start
  957.7 13.8 collective-permute-start
  1027.7 44.6 %collective-permute-start.1 = (bf16[512,768]{1,0:T(8,128)(2,1)}, bf16[512,768]{1,0:T(8,128)(2,1)}, u32[]{:S(2)}, u32[]{:S(2)}) collective-permute-start(bf16[512,768]{1,0:T(8,128)(2,1)} %add_convert_fusion.7), channel_id=1, source_target_pairs={{1,0},{2,1},{3,2},{4,3},{5,4},{6,5},{7,6},{9,8},{10,9},{11,10},{12... | collective-permute-start | bytes 2359304 | tf_op jit(solution)/shard_map/while/body/eval_jaxpr/ppermute | solution.py:78
  1096.0 44.6 %collective-permute-start.1 = (bf16[512,768]{1,0:T(8,128)(2,1)}, bf16[512,768]{1,0:T(8,128)(2,1)}, u32[]{:S(2)}, u32[]{:S(2)}) collective-permute-start(bf16[512,768]{1,0:T(8,128)(2,1)} %add_convert_fusion.7), channel_id=1, source_target_pairs={{1,0},{2,1},{3,2},{4,3},{5,4},{6,5},{7,6},{9,8},{10,9},{11,10},{12... | collective-permute-start | bytes 2359304 | tf_op jit(solution)/shard_map/while/body/eval_jaxpr/ppermute | solution.py:78
  1164.3 44.6 %collective-permute-start.1 = (bf16[512,768]{1,0:T(8,128)(2,1)}, bf16[512,768]{1,0:T(8,128)(2,1)}, u32[]{:S(2)}, u32[]{:S(2)}) collective-permute-start(bf16[512,768]{1,0:T(8,128)(2,1)} %add_convert_fusion.7), channel_id=1, source_target_pairs={{1,0},{2,1},{3,2},{4,3},{5,4},{6,5},{7,6},{9,8},{10,9},{11,10},{12... | collective-permute-start | bytes 2359304 | tf_op jit(solution)/shard_map/while/body/eval_jaxpr/ppermute | solution.py:78
  1232.5 44.6 %collective-permute-start.1 = (bf16[512,768]{1,0:T(8,128)(2,1)}, bf16[512,768]{1,0:T(8,128)(2,1)}, u32[]{:S(2)}, u32[]{:S(2)}) collective-permute-start(bf16[512,768]{1,0:T(8,128)(2,1)} %add_convert_fusion.7), channel_id=1, source_target_pairs={{1,0},{2,1},{3,2},{4,3},{5,4},{6,5},{7,6},{9,8},{10,9},{11,10},{12... | collective-permute-start | bytes 2359304 | tf_op jit(solution)/shard_map/while/body/eval_jaxpr/ppermute | solution.py:78
  1300.8 44.6 %collective-permute-start.1 = (bf16[512,768]{1,0:T(8,128)(2,1)}, bf16[512,768]{1,0:T(8,128)(2,1)}, u32[]{:S(2)}, u32[]{:S(2)}) collective-permute-start(bf16[512,768]{1,0:T(8,128)(2,1)} %add_convert_fusion.7), channel_id=1, source_target_pairs={{1,0},{2,1},{3,2},{4,3},{5,4},{6,5},{7,6},{9,8},{10,9},{11,10},{12... | collective-permute-start | bytes 2359304 | tf_op jit(solution)/shard_map/while/body/eval_jaxpr/ppermute | solution.py:78
  1369.1 44.6 %collective-permute-start.1 = (bf16[512,768]{1,0:T(8,128)(2,1)}, bf16[512,768]{1,0:T(8,128)(2,1)}, u32[]{:S(2)}, u32[]{:S(2)}) collective-permute-start(bf16[512,768]{1,0:T(8,128)(2,1)} %add_convert_fusion.7), channel_id=1, source_target_pairs={{1,0},{2,1},{3,2},{4,3},{5,4},{6,5},{7,6},{9,8},{10,9},{11,10},{12... | collective-permute-start | bytes 2359304 | tf_op jit(solution)/shard_map/while/body/eval_jaxpr/ppermute | solution.py:78
  1437.3 44.6 %collective-permute-start.1 = (bf16[512,768]{1,0:T(8,128)(2,1)}, bf16[512,768]{1,0:T(8,128)(2,1)}, u32[]{:S(2)}, u32[]{:S(2)}) collective-permute-start(bf16[512,768]{1,0:T(8,128)(2,1)} %add_convert_fusion.7), channel_id=1, source_target_pairs={{1,0},{2,1},{3,2},{4,3},{5,4},{6,5},{7,6},{9,8},{10,9},{11,10},{12... | collective-permute-start | bytes 2359304 | tf_op jit(solution)/shard_map/while/body/eval_jaxpr/ppermute | solution.py:78
  1505.6 44.6 %collective-permute-start.1 = (bf16[512,768]{1,0:T(8,128)(2,1)}, bf16[512,768]{1,0:T(8,128)(2,1)}, u32[]{:S(2)}, u32[]{:S(2)}) collective-permute-start(bf16[512,768]{1,0:T(8,128)(2,1)} %add_convert_fusion.7), channel_id=1, source_target_pairs={{1,0},{2,1},{3,2},{4,3},{5,4},{6,5},{7,6},{9,8},{10,9},{11,10},{12... | collective-permute-start | bytes 2359304 | tf_op jit(solution)/shard_map/while/body/eval_jaxpr/ppermute | solution.py:78
  1573.9 44.9 %collective-permute-start.1 = (bf16[512,768]{1,0:T(8,128)(2,1)}, bf16[512,768]{1,0:T(8,128)(2,1)}, u32[]{:S(2)}, u32[]{:S(2)}) collective-permute-start(bf16[512,768]{1,0:T(8,128)(2,1)} %add_convert_fusion.7), channel_id=1, source_target_pairs={{1,0},{2,1},{3,2},{4,3},{5,4},{6,5},{7,6},{9,8},{10,9},{11,10},{12... | collective-permute-start | bytes 2359304 | tf_op jit(solution)/shard_map/while/body/eval_jaxpr/ppermute | solution.py:78
  1642.5 44.9 %collective-permute-start.1 = (bf16[512,768]{1,0:T(8,128)(2,1)}, bf16[512,768]{1,0:T(8,128)(2,1)}, u32[]{:S(2)}, u32[]{:S(2)}) collective-permute-start(bf16[512,768]{1,0:T(8,128)(2,1)} %add_convert_fusion.7), channel_id=1, source_target_pairs={{1,0},{2,1},{3,2},{4,3},{5,4},{6,5},{7,6},{9,8},{10,9},{11,10},{12... | collective-permute-start | bytes 2359304 | tf_op jit(solution)/shard_map/while/body/eval_jaxpr/ppermute | solution.py:78
  1711.1 44.6 %collective-permute-start.1 = (bf16[512,768]{1,0:T(8,128)(2,1)}, bf16[512,768]{1,0:T(8,128)(2,1)}, u32[]{:S(2)}, u32[]{:S(2)}) collective-permute-start(bf16[512,768]{1,0:T(8,128)(2,1)} %add_convert_fusion.7), channel_id=1, source_target_pairs={{1,0},{2,1},{3,2},{4,3},{5,4},{6,5},{7,6},{9,8},{10,9},{11,10},{12... | collective-permute-start | bytes 2359304 | tf_op jit(solution)/shard_map/while/body/eval_jaxpr/ppermute | solution.py:78
  1779.3 44.9 %collective-permute-start.1 = (bf16[512,768]{1,0:T(8,128)(2,1)}, bf16[512,768]{1,0:T(8,128)(2,1)}, u32[]{:S(2)}, u32[]{:S(2)}) collective-permute-start(bf16[512,768]{1,0:T(8,128)(2,1)} %add_convert_fusion.7), channel_id=1, source_target_pairs={{1,0},{2,1},{3,2},{4,3},{5,4},{6,5},{7,6},{9,8},{10,9},{11,10},{12... | collective-permute-start | bytes 2359304 | tf_op jit(solution)/shard_map/while/body/eval_jaxpr/ppermute | solution.py:78
  1847.9 44.6 %collective-permute-start.1 = (bf16[512,768]{1,0:T(8,128)(2,1)}, bf16[512,768]{1,0:T(8,128)(2,1)}, u32[]{:S(2)}, u32[]{:S(2)}) collective-permute-start(bf16[512,768]{1,0:T(8,128)(2,1)} %add_convert_fusion.7), channel_id=1, source_target_pairs={{1,0},{2,1},{3,2},{4,3},{5,4},{6,5},{7,6},{9,8},{10,9},{11,10},{12... | collective-permute-start | bytes 2359304 | tf_op jit(solution)/shard_map/while/body/eval_jaxpr/ppermute | solution.py:78
  1916.2 44.9 %collective-permute-start.1 = (bf16[512,768]{1,0:T(8,128)(2,1)}, bf16[512,768]{1,0:T(8,128)(2,1)}, u32[]{:S(2)}, u32[]{:S(2)}) collective-permute-start(bf16[512,768]{1,0:T(8,128)(2,1)} %add_convert_fusion.7), channel_id=1, source_target_pairs={{1,0},{2,1},{3,2},{4,3},{5,4},{6,5},{7,6},{9,8},{10,9},{11,10},{12... | collective-permute-start | bytes 2359304 | tf_op jit(solution)/shard_map/while/body/eval_jaxpr/ppermute | solution.py:78
  1984.8 44.6 %collective-permute-start.1 = (bf16[512,768]{1,0:T(8,128)(2,1)}, bf16[512,768]{1,0:T(8,128)(2,1)}, u32[]{:S(2)}, u32[]{:S(2)}) collective-permute-start(bf16[512,768]{1,0:T(8,128)(2,1)} %add_convert_fusion.7), channel_id=1, source_target_pairs={{1,0},{2,1},{3,2},{4,3},{5,4},{6,5},{7,6},{9,8},{10,9},{11,10},{12... | collective-permute-start | bytes 2359304 | tf_op jit(solution)/shard_map/while/body/eval_jaxpr/ppermute | solution.py:78
  (190 other events, 2030.3 us)
Sparse Core Ops, SparseCore 0:
  2029.6 862.5 all-reduce.2
where the time goes:
time: 2940 us; the launch traced here: 2920 us
  matrix products  1490 us (51%)
  waiting for transfers between devices  794 us (27%)
  local copies, waits for them, and re-layouts  242 us (8%)
  starting transfers between devices  169 us (6%)
  other arithmetic  124 us (4%)
  blocking collectives  69.2 us (2%)
    psum x1, waiting for transfers between devices, body(): dw1 = lax.psum(dw1, 'dp')  793 us
    dot_general x30, matrix products, bwd_step(): dw2 = dw2.at[j].add(jnp.dot(a.T, g, preferred_element_type=jnp.float32))  366 us
    dot_general x30, matrix products, bwd_step(): dw1 = dw1.at[j].add(jnp.dot(h.T, e, preferred_element_type=jnp.float32))  285 us
    dot_general x30, matrix products, fwd_step(): jnp.dot(h, w1[j], preferred_element_type=jnp.float32).astype(jnp.bfloat16)  258 us
    dot_general x30, matrix products, fwd_step(): jnp.dot(a, w2[j], preferred_element_type=jnp.float32)  249 us
    dot_general x30, matrix products, bwd_step(): q = jnp.dot(g, w2[j].T, preferred_element_type=jnp.float32)  235 us
    ppermute x15, starting transfers between devices, fwd_step(): recv = lax.ppermute(h, 'pp', down)  150 us
    dot_general x30, matrix products, bwd_step(): jnp.dot(e, w1[j].T, preferred_element_type=jnp.float32)  93.7 us
  transfers between devices with their start and end apart: 31, of which 1 were waited for; matrix products, arithmetic and copies ran while one was open for 23% of the time, Pallas kernels for 0%

commit v1 on v0

v1 whole, which is shorter than its diff:
```python
import functools
import math

import jax
import jax.numpy as jnp
from jax import lax
from jax.experimental import pallas as pl
from jax.experimental.pallas import tpu as pltpu
from jax.sharding import PartitionSpec as P

MESH = pl.DeviceIdType.MESH
BF, F32 = jnp.bfloat16, jnp.float32
ANY = pl.BlockSpec(memory_space=pl.ANY)
C0 = math.sqrt(2.0 / math.pi)
C1 = C0 * 0.044715
T = 256
CH = 768


def _nn(a, b):
    return jnp.dot(a, b, preferred_element_type=F32)


def _nt(a, b):
    return lax.dot_general(a, b, (((1,), (1,)), ((), ())), preferred_element_type=F32)


def _tn(a, b):
    return lax.dot_general(a, b, (((0,), (0,)), ((), ())), preferred_element_type=F32)


def _layer(x, n, first, point, second):
    r = x.astype(F32)
    q = first(x, 0)
    for c in range(n):
        ahead = first(x, c + 1) if c + 1 < n else None
        a = point(q, c)
        if second is not None:
            r = r + second(a, c)
        q = ahead
    return None if second is None else r.astype(BF)


def _stage_kernel(ndp, npp, nb, inv, x_ref, t_ref, w1_ref, w2_ref,
                  h_out, g_out, a_out, e_out, loss_out,
                  w1, w2, hin, gin, us, as_, ub, es, h1s, g0s, hst, gst, acc,
                  wsem, hrecv, grecv, xhrecv, xgrecv, zhsend, zgsend, hcp, gcp, h1sem, g0sem,
                  ussem, assem, ubsem, essem, hsend, gsend, lsend, lrecv):
    z = lax.axis_index("dp")
    s = lax.axis_index("pp")
    peer = (1 - z, s)
    ff = w1.shape[-1]
    nc = ff // CH
    first, last = s == 0, s == npp - 1

    loads = []
    for j in range(2):
        for k, (src, dst) in enumerate(((w1_ref, w1), (w2_ref, w2))):
            loads.append(pltpu.make_async_copy(src.at[j], dst.at[j], wsem.at[j, k]))
    for c in loads:
        c.start()

    barrier = pltpu.get_barrier_semaphore()
    for dz in range(ndp):
        for ds in range(npp):
            if dz or ds:
                pl.semaphore_signal(barrier, inc=1, device_id=((z + dz) % ndp, (s + ds) % npp), device_id_type=MESH)
    pl.semaphore_wait(barrier, ndp * npp - 1)

    def x_copy(m):
        return pltpu.make_async_copy(x_ref.at[m], hin.at[0, m], hrecv.at[m])

    def t_copy(m):
        return pltpu.make_async_copy(t_ref.at[m], gin.at[0, m], grecv.at[m])

    def each(n, f):
        def step(i, c):
            f(i)
            return c
        lax.fori_loop(0, n, step, 0)

    @pl.when(first)
    def _():
        each(nb, lambda m: x_copy(m).start())

    @pl.when(last)
    def _():
        each(nb, lambda m: t_copy(m).start())
        acc[...] = jnp.zeros_like(acc)

    def share(buf, m, send, recv):
        return pltpu.make_async_remote_copy(src_ref=buf.at[0, m], dst_ref=buf.at[1, m], send_sem=send.at[m], recv_sem=recv.at[m],
                                            device_id=peer, device_id_type=MESH)

    def pass_h(m, k):
        return pltpu.make_async_remote_copy(src_ref=hst.at[k], dst_ref=hin.at[0, m], send_sem=hsend.at[k], recv_sem=hrecv.at[m],
                                            device_id=(z, lax.rem(s + 1, npp)), device_id_type=MESH)

    def pass_g(m, k):
        return pltpu.make_async_remote_copy(src_ref=gst.at[k], dst_ref=gin.at[0, m], send_sem=gsend.at[k], recv_sem=grecv.at[m],
                                            device_id=(z, lax.rem(s + npp - 1, npp)), device_id_type=MESH)

    def u_out(j, r, m):
        return pltpu.make_async_copy(us.at[j], e_out.at[j, r, m], ussem.at[j])

    def a_outc(j, r, m):
        return pltpu.make_async_copy(as_.at[j], a_out.at[j, r, m], assem.at[j])

    def u_in(j, r, m):
        return pltpu.make_async_copy(e_out.at[j, r, m], ub.at[j], ubsem.at[j])

    def e_outc(j, r, m):
        return pltpu.make_async_copy(es.at[j], e_out.at[j, r, m], essem.at[j])

    def keep(src, dst, sem):
        return pltpu.make_async_copy(src, dst, sem)

    def gelu(j):
        def point(q, c):
            cs = pl.ds(c * CH, CH)
            u = q.astype(BF)
            us[j, :, cs] = u
            u = u.astype(F32)
            hu = 0.5 * u
            a = (hu + hu * jnp.tanh(u * (C0 + C1 * (u * u)))).astype(BF)
            as_[j, :, cs] = a
            return a
        return point

    def dgelu(j):
        def point(q, c):
            cs = pl.ds(c * CH, CH)
            u = ub[j, :, cs].astype(F32)
            u2 = u * u
            th = jnp.tanh(u * (C0 + C1 * u2))
            d = (0.5 + 0.5 * th) + (u * (0.5 * C0 + (1.5 * C1) * u2)) * (1.0 - th * th)
            e = (d * q).astype(BF)
            es[j, :, cs] = e
            return e
        return point

    def fwd(j, x, full=True):
        second = (lambda a, c: _nn(a, w2[j, pl.ds(c * CH, CH), :])) if full else None
        return _layer(x, nc, lambda x, c: _nn(x, w1[j, :, pl.ds(c * CH, CH)]), gelu(j), second)

    def bwd(j, g, full=True):
        second = (lambda e, c: _nt(e, w1[j, :, pl.ds(c * CH, CH)])) if full else None
        return _layer(g, nc, lambda g, c: _nt(g, w2[j, pl.ds(c * CH, CH), :]), dgelu(j), second)

    def drain_f():
        for j in range(2):
            u_out(j, 0, 0).wait()
            a_outc(j, 0, 0).wait()

    def fwd_task(o, m, idle):
        r = z if o == 0 else 1 - z
        if o == 0:
            x_copy(m).wait()
            share(hin, m, zhsend, xhrecv).start()
        else:
            share(hin, m, zhsend, xhrecv).wait_recv()
        keep(hin.at[o, m], h_out.at[0, r, m], hcp).start()

        @pl.when(jnp.logical_not(idle))
        def _():
            u_out(0, 0, 0).wait()
            a_outc(0, 0, 0).wait()

        if o == 0:
            @pl.when(m == 0)
            def _():
                loads[0].wait()
                loads[1].wait()

            @pl.when(m > 0)
            def _():
                keep(h1s, h_out.at[1, r, m], h1sem).wait()
        else:
            keep(h1s, h_out.at[1, r, m], h1sem).wait()
        h1s[...] = fwd(0, hin[o, m])
        u_out(0, r, m).start()
        a_outc(0, r, m).start()
        keep(h1s, h_out.at[1, r, m], h1sem).start()

        @pl.when(jnp.logical_not(idle))
        def _():
            u_out(1, 0, 0).wait()
            a_outc(1, 0, 0).wait()

        if o == 0:
            @pl.when(m == 0)
            def _():
                loads[2].wait()
                loads[3].wait()

            k = m % 2

            @pl.when(jnp.logical_and(m > 1, jnp.logical_not(last)))
            def _():
                pass_h(m, k).wait_send()
            hst[k] = fwd(1, h1s[...])
        else:
            fwd(1, h1s[...], full=False)
        u_out(1, r, m).start()
        a_outc(1, r, m).start()
        if o == 0:
            @pl.when(jnp.logical_not(last))
            def _():
                pass_h(m, k).start()

            @pl.when(last)
            def _():
                t_copy(m).wait()
                d = hst[k].astype(F32) - gin[0, m].astype(F32)
                gin[0, m] = (d * inv).astype(BF)
                p = jnp.sum((d * d).reshape(T // 8, 8, d.shape[-1]), axis=0)
                acc[...] += sum(p[:, i:i + 128] for i in range(0, d.shape[-1], 128))

    def bwd_task(o, m, b):
        r = z if o == 0 else 1 - z
        if o == 0:
            @pl.when(jnp.logical_not(last))
            def _():
                t_copy(m).wait()
            share(gin, m, zgsend, xgrecv).start()
        else:
            share(gin, m, zgsend, xgrecv).wait_recv()
        keep(gin.at[o, m], g_out.at[1, r, m], gcp).start()

        def ready(j):
            @pl.when(b > 0)
            def _():
                e_outc(j, 0, 0).wait()
                if j == 1:
                    keep(g0s, g_out.at[0, r, m], g0sem).wait()
            u_in(j, r, m).wait()

        def ahead(j):
            @pl.when(m + 1 < nb)
            def _():
                u_in(j, r, m + 1).start()

        ready(1)
        g0s[...] = bwd(1, gin[o, m])
        e_outc(1, r, m).start()
        keep(g0s, g_out.at[0, r, m], g0sem).start()
        ahead(1)
        ready(0)
        if o == 0:
            k = m % 2

            @pl.when(jnp.logical_and(m > 1, jnp.logical_not(first)))
            def _():
                pass_g(m, k).wait_send()
            gst[k] = bwd(0, g0s[...])
        else:
            bwd(0, g0s[...], full=False)
        e_outc(0, r, m).start()
        ahead(0)
        if o == 0:
            @pl.when(jnp.logical_not(first))
            def _():
                pass_g(m, k).start()

    room = jnp.minimum(nb, (8 * (npp - 1 - s)) // 3)

    def task(i, c):
        @pl.when(i < nb)
        def _():
            fwd_task(0, i, i == 0)

        early = jnp.logical_and(i >= nb, i < nb + room)
        late = jnp.logical_and(i >= 2 * nb + room, i < 3 * nb)

        @pl.when(jnp.logical_or(early, late))
        def _():
            m = jnp.where(early, i - nb, i - 2 * nb)
            fwd_task(1, m, m == 0)

        @pl.when(jnp.logical_and(i >= nb + room, i < 2 * nb + room))
        def _():
            m = i - nb - room
            bwd_task(0, m, m)

        @pl.when(i >= 3 * nb)
        def _():
            m = i - 3 * nb
            bwd_task(1, m, m + nb)

        for end, r in ((nb - 1, z), (3 * nb - 1, 1 - z)):
            @pl.when(i == end)
            def _():
                drain_f()
                for j in (1, 0):
                    u_in(j, r, 0).start()
        return c

    lax.fori_loop(0, 4 * nb, task, 0)

    def loss_copy(dz, ds):
        return pltpu.make_async_remote_copy(src_ref=acc, dst_ref=loss_out.at[z], send_sem=lsend.at[dz * npp + ds],
                                            recv_sem=lrecv.at[z],
                                            device_id=((z + dz) % ndp, (s + ds) % npp), device_id_type=MESH)

    def loss_own():
        return pltpu.make_async_copy(acc, loss_out.at[z], lrecv.at[z])

    @pl.when(last)
    def _():
        loss_own().start()
        for dz in range(ndp):
            for ds in range(npp):
                if dz or ds:
                    loss_copy(dz, ds).start()
        for dz in range(ndp):
            for ds in range(npp):
                if dz or ds:
                    loss_copy(dz, ds).wait_send()
    for d in range(ndp):
        pltpu.make_async_copy(acc, loss_out.at[d], lrecv.at[d]).wait()

    def sent(m):
        share(hin, m, zhsend, xhrecv).wait_send()
        share(gin, m, zgsend, xgrecv).wait_send()
    each(nb, sent)
    for k in range(2):
        @pl.when(jnp.logical_not(last))
        def _():
            pass_h(0, k).wait_send()

        @pl.when(jnp.logical_not(first))
        def _():
            pass_g(0, k).wait_send()
    keep(hin, h_out.at[0], hcp).wait()
    keep(gin, g_out.at[1], gcp).wait()
    keep(h1s, h_out.at[1, 0, 0], h1sem).wait()
    keep(g0s, g_out.at[0, 0, 0], g0sem).wait()
    for j in range(2):
        e_outc(j, 0, 0).wait()


def _stages(x, t, w1, w2, ndp, npp, inv):
    nb, _, d = x.shape
    ff = w1.shape[-1]
    dma = pltpu.SemaphoreType.DMA
    act = jax.ShapeDtypeStruct((2, ndp, nb, T, d), BF)
    wide = jax.ShapeDtypeStruct((2, ndp, nb, T, ff), BF)
    flops = 28 * nb * T * d * ff
    return pl.pallas_call(
        functools.partial(_stage_kernel, ndp, npp, nb, inv),
        out_shape=(act, act, wide, wide, jax.ShapeDtypeStruct((ndp, 8, 128), F32)),
        in_specs=[ANY] * 4,
        out_specs=(ANY,) * 5,
        scratch_shapes=[
            pltpu.VMEM((2, d, ff), BF), pltpu.VMEM((2, ff, d), BF),
            pltpu.VMEM((ndp, nb, T, d), BF), pltpu.VMEM((ndp, nb, T, d), BF),
            pltpu.VMEM((2, T, ff), BF), pltpu.VMEM((2, T, ff), BF), pltpu.VMEM((2, T, ff), BF), pltpu.VMEM((2, T, ff), BF),
            pltpu.VMEM((T, d), BF), pltpu.VMEM((T, d), BF), pltpu.VMEM((2, T, d), BF), pltpu.VMEM((2, T, d), BF),
            pltpu.VMEM((8, 128), F32),
            dma((2, 2)), dma((nb,)), dma((nb,)), dma((nb,)), dma((nb,)), dma((nb,)), dma((nb,)), dma, dma, dma, dma,
            dma((2,)), dma((2,)), dma((2,)), dma((2,)), dma((2,)), dma((2,)), dma((ndp * npp,)), dma((ndp,)),
        ],
        compiler_params=pltpu.CompilerParams(collective_id=0, has_side_effects=True, vmem_limit_bytes=67_043_328),
        cost_estimate=pl.CostEstimate(flops=flops, bytes_accessed=16 * nb * T * ff, transcendentals=8 * nb * T * ff),
        name="stage",
    )(x, t, w1, w2)


def _dw_kernel(a_ref, b_ref, o_ref):
    o_ref[...] = _tn(a_ref[...], b_ref[...])


def _dw(a, b, wide_left):
    n, tokens, p = a.shape
    q = b.shape[-1]
    tile = 512
    whole = lambda w: pl.BlockSpec((None, tokens, w), lambda j, i: (j, 0, 0))
    part = pl.BlockSpec((None, tokens, tile), lambda j, i: (j, 0, i))
    if wide_left:
        grid, specs, out = (n, p // tile), [part, whole(q)], pl.BlockSpec((None, tile, q), lambda j, i: (j, i, 0))
    else:
        grid, specs, out = (n, q // tile), [whole(p), part], pl.BlockSpec((None, p, tile), lambda j, i: (j, 0, i))
    return pl.pallas_call(
        _dw_kernel,
        grid=grid,
        out_shape=jax.ShapeDtypeStruct((n, p, q), F32),
        in_specs=specs,
        out_specs=out,
        compiler_params=pltpu.CompilerParams(vmem_limit_bytes=62 * 1024 * 1024),
        cost_estimate=pl.CostEstimate(flops=2 * n * tokens * p * q, bytes_accessed=4 * n * tokens * q, transcendentals=0),
    )(a, b)


def solution(mesh):
    ndp = mesh.shape["dp"]
    npp = mesh.shape["pp"]

    def body(x, t, w1, w2):
        nm, tok, d = x.shape
        ff = w1.shape[-1]
        inv = 1.0 / (nm * tok * ndp * d)
        nb = nm * tok // T
        h, g, a, e, loss = _stages(x.reshape(nb, T, d), t.reshape(nb, T, d), w1[0], w2[0], ndp, npp, inv)
        n = ndp * nb * T
        dw1 = _dw(h.reshape(2, n, d), e.reshape(2, n, ff), False)
        dw2 = _dw(a.reshape(2, n, ff), g.reshape(2, n, d), True)
        return dw1[None], dw2[None], 0.5 * inv * jnp.sum(loss)

    return jax.shard_map(body, mesh=mesh,
                         in_specs=(P(None, 'dp', None), P(None, 'dp', None), P('pp'), P('pp')),
                         out_specs=(P('pp'), P('pp'), P()), check_vma=False)
```

time: 2940 us -> 613 us (0.21)
  matrix products: 1490 us -> 0 us
  waiting for transfers between devices: 794 us -> 0 us
  Pallas kernels: 0 us -> 609 us
  local copies, waits for them, and re-layouts: 242 us -> 0 us
  starting transfers between devices: 169 us -> 0 us
  other arithmetic: 124 us -> 1.3 us
  blocking collectives: 69.2 us -> 0 us
    dot_general x180 -> x0, matrix products: 1490 us -> none  [the longest x30 366 us: bwd_step(): dw2 = dw2.at[j].add(jnp.dot(a.T, g, preferred_element_type=jnp.float32))]
    psum x1 -> x0, waiting for transfers between devices: 793 us -> none  [body(): dw1 = lax.psum(dw1, 'dp')]
    pallas_call x0 -> x3, Pallas kernels: none -> 609 us  [the longest x1 430 us: _stages(): pl.pallas_call(functools.partial(_stage_kernel, ndp, npp, nb, inv), out_s...]
    dynamic_slice x75 -> x0, local copies, waits for them, and re-layouts: 172 us -> none  [the longest x30 87.8 us: fwd_step(): ubuf = ubuf.at[j, mc].set(jnp.where(valid, u, ubuf[j, mc]))]
    ppermute x30 -> x0, starting transfers between devices: 169 us -> none  [the longest x15 150 us: fwd_step(): recv = lax.ppermute(h, 'pp', down)]
    psum x1 -> x0, blocking collectives: 69.2 us -> none  [body(): loss = lax.psum(lsum * inv, ('dp', 'pp'))]
    scatter x15 -> x0, other arithmetic: 45.3 us -> none  [fwd_step(): hbuf = hbuf.at[j, mc].set(jnp.where(valid, h, hbuf[j, mc]))]
    broadcast_in_dim x5 -> x0, local copies, waits for them, and re-layouts: 42.3 us -> none  [the longest x1 16.3 us: body(): jnp.zeros((2, nm, tok, ff), jnp.bfloat16)]
  transfers between devices with their start and end apart: 31 -> 0, of which waited for: 1 -> 0; matrix products, arithmetic and copies ran while one was open for 23% -> 0% of each run, Pallas kernels for 0% -> 0%
where the time goes in v1:
time: 613 us
  Pallas kernels  609 us (99%)
    pallas_call x1, Pallas kernels, _stages(): pl.pallas_call(functools.partial(_stage_kernel, ndp, npp, nb, inv), out_s...  430 us
    pallas_call x2, Pallas kernels, _dw(): pl.pallas_call(_dw_kernel, grid=grid, out_shape=jax.ShapeDtypeStruct((n,...  179 us

profile of v1, /device:TPU:0, one launch (start us, length us, event | category | flops | bytes accessed | tf_op | source)
XLA Modules:
  0.0 613.0 jit_solution(9223819709600957666)
XLA Ops:
  0.6 430.4 %stage.1 = (bf16[2,2,16,256,768]{4,3,2,1,0:T(8,128)(2,1)}, bf16[2,2,16,256,768]{4,3,2,1,0:T(8,128)(2,1)}, bf16[2,2,16,256,3072]{4,3,2,1,0:T(8,128)(2,1)}, bf16[2...) custom-call(bf16[16,256,768]{2,1,0:T(8,128)(2,1)} %bitcast.12, bf16[16,256,768]{2,1,0:T(8,128)(2,1)} %bitcast.13, ...), custom_call_target="tpu_custom_call" | custom-call | flops 270582939648 | bytes 201326592 | tf_op jit(solution)/shard_map/stage/pallas_call | solution.py:349
  431.1 1.3 reduce_sum.9
  433.0 89.3 %shard_map.67 = f32[2,768,3072]{2,1,0:T(8,128)} custom-call(bf16[2,8192,768]{2,1,0:T(8,128)(2,1)} %bitcast.15, bf16[2,8192,3072]{2,1,0:T(8,128)(2,1)} %bitcast.5.b_ref), custom_call_target="tpu_custom_call" | custom-call | flops 77309411328 | bytes 201326592 | tf_op jit(solution)/shard_map/pallas_call | solution.py:383
  522.3 89.6 %shard_map.68 = f32[2,3072,768]{2,1,0:T(8,128)} custom-call(bf16[2,8192,3072]{2,1,0:T(8,128)(2,1)} %bitcast.7.a_ref, bf16[2,8192,768]{2,1,0:T(8,128)(2,1)} %bitcast.14), custom_call_target="tpu_custom_call" | custom-call | flops 77309411328 | bytes 50331648 | tf_op jit(solution)/shard_map/pallas_call | solution.py:383

commit v2 on v1

v2 whole, which is shorter than its diff:
```python
import functools
import math

import jax
import jax.numpy as jnp
from jax import lax
from jax.experimental import pallas as pl
from jax.experimental.pallas import tpu as pltpu
from jax.sharding import PartitionSpec as P

MESH = pl.DeviceIdType.MESH
BF, F32 = jnp.bfloat16, jnp.float32
ANY = pl.BlockSpec(memory_space=pl.ANY)
C0 = math.sqrt(2.0 / math.pi)
C1 = C0 * 0.044715
T = 256
TF = 128
CH = 768


def _nn(a, b):
    return jnp.dot(a, b, preferred_element_type=F32)


def _nt(a, b):
    return lax.dot_general(a, b, (((1,), (1,)), ((), ())), preferred_element_type=F32)


def _tn(a, b):
    return lax.dot_general(a, b, (((0,), (0,)), ((), ())), preferred_element_type=F32)


def _layer(x, n, first, point, second):
    r = x.astype(F32)
    q = first(x, 0)
    for c in range(n):
        ahead = first(x, c + 1) if c + 1 < n else None
        a = point(q, c)
        if second is not None:
            r = r + second(a, c)
        q = ahead
    return None if second is None else r.astype(BF)


def _stage_kernel(ndp, npp, nb, inv, x_ref, t_ref, w1_ref, w2_ref,
                  h_out, g_out, a_out, e_out, loss_out,
                  w1, w2, hin, gin, us, as_, ub, es, h1s, g0s, hst, gst, acc,
                  wsem, hrecv, grecv, xhrecv, xgrecv, zhsend, zgsend, hcp, gcp, h1sem, g0sem,
                  ussem, assem, ubsem, essem, hsend, gsend, lsend, lrecv):
    z = lax.axis_index("dp")
    s = lax.axis_index("pp")
    peer = (1 - z, s)
    ff = w1.shape[-1]
    nc = ff // CH
    first, last = s == 0, s == npp - 1

    loads = []
    for j in range(2):
        for k, (src, dst) in enumerate(((w1_ref, w1), (w2_ref, w2))):
            loads.append(pltpu.make_async_copy(src.at[j], dst.at[j], wsem.at[j, k]))
    for c in loads:
        c.start()

    barrier = pltpu.get_barrier_semaphore()
    for dz in range(ndp):
        for ds in range(npp):
            if dz or ds:
                pl.semaphore_signal(barrier, inc=1, device_id=((z + dz) % ndp, (s + ds) % npp), device_id_type=MESH)
    pl.semaphore_wait(barrier, ndp * npp - 1)

    per = T // TF

    def part(i):
        return lax.div(i, per), pl.ds(pl.multiple_of(lax.rem(i, per) * TF, TF), TF)

    def x_copy(i):
        return pltpu.make_async_copy(x_ref.at[part(i)], hin.at[0, *part(i)], hrecv.at[i])

    def t_copy(m):
        return pltpu.make_async_copy(t_ref.at[m], gin.at[0, m], grecv.at[m])

    def each(n, f):
        def step(i, c):
            f(i)
            return c
        lax.fori_loop(0, n, step, 0)

    @pl.when(first)
    def _():
        each(per * nb, lambda i: x_copy(i).start())

    @pl.when(last)
    def _():
        each(nb, lambda m: t_copy(m).start())
        acc[...] = jnp.zeros_like(acc)

    def share_h(i):
        return pltpu.make_async_remote_copy(src_ref=hin.at[0, *part(i)], dst_ref=hin.at[1, *part(i)], send_sem=zhsend.at[i],
                                            recv_sem=xhrecv.at[i], device_id=peer, device_id_type=MESH)

    def share_g(m):
        return pltpu.make_async_remote_copy(src_ref=gin.at[0, m], dst_ref=gin.at[1, m], send_sem=zgsend.at[m],
                                            recv_sem=xgrecv.at[m], device_id=peer, device_id_type=MESH)

    def pass_h(i, k):
        return pltpu.make_async_remote_copy(src_ref=hst.at[k], dst_ref=hin.at[0, *part(i)], send_sem=hsend.at[k],
                                            recv_sem=hrecv.at[i], device_id=(z, lax.rem(s + 1, npp)), device_id_type=MESH)

    def pass_g(m, k):
        return pltpu.make_async_remote_copy(src_ref=gst.at[k], dst_ref=gin.at[0, m], send_sem=gsend.at[k], recv_sem=grecv.at[m],
                                            device_id=(z, lax.rem(s + npp - 1, npp)), device_id_type=MESH)

    def f_out(j, r, m):
        return (pltpu.make_async_copy(us.at[j], e_out.at[j, r, m], ussem.at[j, 0]),
                pltpu.make_async_copy(as_.at[j], a_out.at[j, r, m], assem.at[j, 0]))

    def f_out_part(j, i, k):
        m, rows = part(i)
        mine = pl.ds(pl.multiple_of(k * TF, TF), TF)
        return (pltpu.make_async_copy(us.at[j, mine], e_out.at[j, z, m, rows], ussem.at[j, k]),
                pltpu.make_async_copy(as_.at[j, mine], a_out.at[j, z, m, rows], assem.at[j, k]))

    def u_in(j, r, m):
        return pltpu.make_async_copy(e_out.at[j, r, m], ub.at[j], ubsem.at[j])

    def e_outc(j, r, m):
        return pltpu.make_async_copy(es.at[j], e_out.at[j, r, m], essem.at[j])

    def keep(src, dst, sem):
        return pltpu.make_async_copy(src, dst, sem)

    def gelu(j, rows):
        def point(q, c):
            cs = pl.ds(c * CH, CH)
            u = q.astype(BF)
            us[j, rows, cs] = u
            u = u.astype(F32)
            a = ((0.5 * u) * (1.0 + jnp.tanh(u * (C0 + C1 * (u * u))))).astype(BF)
            as_[j, rows, cs] = a
            return a
        return point

    def dgelu(j):
        def point(q, c):
            cs = pl.ds(c * CH, CH)
            u = jnp.clip(ub[j, :, cs], -30.0, 30.0).astype(F32)
            k = C1 * (u * u)
            th = jnp.tanh(u * (C0 + k))
            d = (1.0 + th) * (0.5 + (1.0 - th) * (u * (0.5 * C0 + 1.5 * k)))
            e = (d * q).astype(BF)
            es[j, :, cs] = e
            return e
        return point

    def fwd(j, x, rows, full=True):
        second = (lambda a, c: _nn(a, w2[j, pl.ds(c * CH, CH), :])) if full else None
        return _layer(x, nc, lambda x, c: _nn(x, w1[j, :, pl.ds(c * CH, CH)]), gelu(j, rows), second)

    def bwd(j, g, full=True):
        second = (lambda e, c: _nt(e, w1[j, :, pl.ds(c * CH, CH)])) if full else None
        return _layer(g, nc, lambda g, c: _nt(g, w2[j, pl.ds(c * CH, CH), :]), dgelu(j), second)

    def start(copies):
        for c in copies:
            c.start()

    def wait(copies):
        for c in copies:
            c.wait()

    def fwd_own(i):
        m, rows = part(i)
        k = lax.rem(i, 2)
        mine = pl.ds(pl.multiple_of(k * TF, TF), TF)
        x_copy(i).wait()
        share_h(i).start()
        keep(hin.at[0, m, rows], h_out.at[0, z, m, rows], hcp).start()

        @pl.when(i == 0)
        def _():
            wait(loads[:2])

        def h1_out():
            return keep(h1s.at[mine], h_out.at[1, z, m, rows], h1sem.at[k])

        @pl.when(i > 1)
        def _():
            wait(f_out_part(0, i, k))
            h1_out().wait()
        h1s[mine] = fwd(0, hin[0, m, rows], mine)
        start(f_out_part(0, i, k))
        h1_out().start()

        @pl.when(i == 0)
        def _():
            wait(loads[2:])

        @pl.when(i > 1)
        def _():
            wait(f_out_part(1, i, k))

            @pl.when(jnp.logical_not(last))
            def _():
                pass_h(i, k).wait_send()
        hst[k] = fwd(1, h1s[mine], mine)
        start(f_out_part(1, i, k))

        @pl.when(jnp.logical_not(last))
        def _():
            pass_h(i, k).start()

        @pl.when(last)
        def _():
            @pl.when(lax.rem(i, per) == 0)
            def _():
                t_copy(m).wait()
            d = hst[k].astype(F32) - gin[0, m, rows].astype(F32)
            gin[0, m, rows] = (d * inv).astype(BF)
            p = jnp.sum((d * d).reshape(TF // 8, 8, d.shape[-1]), axis=0)
            acc[...] += sum(p[:, c:c + 128] for c in range(0, d.shape[-1], 128))

    def fwd_other(m):
        r = 1 - z
        rows = pl.ds(0, T)
        for p in range(per):
            share_h(per * m + p).wait_recv()
        keep(hin.at[1, m], h_out.at[0, r, m], hcp).start()

        @pl.when(m > 0)
        def _():
            wait(f_out(0, r, m))
            keep(h1s, h_out.at[1, r, m], h1sem.at[0]).wait()
        h1s[...] = fwd(0, hin[1, m], rows)
        start(f_out(0, r, m))
        keep(h1s, h_out.at[1, r, m], h1sem.at[0]).start()

        @pl.when(m > 0)
        def _():
            wait(f_out(1, r, m))
        fwd(1, h1s[...], rows, full=False)
        start(f_out(1, r, m))

    def bwd_task(o, m, b):
        r = z if o == 0 else 1 - z
        if o == 0:
            @pl.when(jnp.logical_not(last))
            def _():
                t_copy(m).wait()
            share_g(m).start()
        else:
            share_g(m).wait_recv()
        keep(gin.at[o, m], g_out.at[1, r, m], gcp).start()

        def ready(j):
            @pl.when(b > 0)
            def _():
                e_outc(j, 0, 0).wait()
                if j == 1:
                    keep(g0s, g_out.at[0, r, m], g0sem).wait()
            u_in(j, r, m).wait()

        def ahead(j):
            @pl.when(m + 1 < nb)
            def _():
                u_in(j, r, m + 1).start()

        ready(1)
        g0s[...] = bwd(1, gin[o, m])
        e_outc(1, r, m).start()
        keep(g0s, g_out.at[0, r, m], g0sem).start()
        ahead(1)
        ready(0)
        if o == 0:
            k = m % 2

            @pl.when(jnp.logical_and(m > 1, jnp.logical_not(first)))
            def _():
                pass_g(m, k).wait_send()
            gst[k] = bwd(0, g0s[...])
        else:
            bwd(0, g0s[...], full=False)
        e_outc(0, r, m).start()
        ahead(0)
        if o == 0:
            @pl.when(jnp.logical_not(first))
            def _():
                pass_g(m, k).start()

    def loss_copy(dz, ds):
        return pltpu.make_async_remote_copy(src_ref=acc, dst_ref=loss_out.at[z], send_sem=lsend.at[dz * npp + ds],
                                            recv_sem=lrecv.at[z],
                                            device_id=((z + dz) % ndp, (s + ds) % npp), device_id_type=MESH)

    def loss_own():
        return pltpu.make_async_copy(acc, loss_out.at[z], lrecv.at[z])

    others = [(dz, ds) for dz in range(ndp) for ds in range(npp) if dz or ds]

    def send_loss():
        loss_own().start()
        for dz, ds in others:
            loss_copy(dz, ds).start()

    room = jnp.minimum(nb, (8 * (npp - 1 - s)) // 3)

    nf = per * nb
    a, b, c, d = nf + room, nf + room + nb, nf + 2 * nb, nf + 3 * nb

    def load_u(r):
        for j in (1, 0):
            u_in(j, r, 0).start()

    def task(i, carry):
        @pl.when(i < nf)
        def _():
            fwd_own(i)

        @pl.when(i == nf - 1)
        def _():
            for j in range(2):
                for k in range(2):
                    wait(f_out_part(j, 0, k))
            for k in range(2):
                keep(h1s.at[pl.ds(k * TF, TF)], h_out.at[1, z, 0, pl.ds(k * TF, TF)], h1sem.at[k]).wait()
            load_u(z)
            pl.when(last)(send_loss)

        early = jnp.logical_and(i >= nf, i < a)
        late = jnp.logical_and(i >= b, i < c)

        @pl.when(jnp.logical_or(early, late))
        def _():
            fwd_other(jnp.where(early, i - nf, i - nf - nb))

        @pl.when(jnp.logical_and(i >= a, i < b))
        def _():
            bwd_task(0, i - a, i - a)

        @pl.when(i == c - 1)
        def _():
            for j in range(2):
                wait(f_out(j, 0, 0))
            load_u(1 - z)

        @pl.when(i >= c)
        def _():
            bwd_task(1, i - c, i - c + nb)
        return carry

    lax.fori_loop(0, d, task, 0)

    @pl.when(last)
    def _():
        for dz, ds in others:
            loss_copy(dz, ds).wait_send()
    for d in range(ndp):
        pltpu.make_async_copy(acc, loss_out.at[d], lrecv.at[d]).wait()
    each(nf, lambda i: share_h(i).wait_send())
    each(nb, lambda m: share_g(m).wait_send())
    for k in range(2):
        @pl.when(jnp.logical_not(last))
        def _():
            pass_h(0, k).wait_send()

        @pl.when(jnp.logical_not(first))
        def _():
            pass_g(0, k).wait_send()
    keep(hin, h_out.at[0], hcp).wait()
    keep(gin, g_out.at[1], gcp).wait()
    keep(h1s, h_out.at[1, 0, 0], h1sem.at[0]).wait()
    keep(g0s, g_out.at[0, 0, 0], g0sem).wait()
    for j in range(2):
        e_outc(j, 0, 0).wait()


def _stages(x, t, w1, w2, ndp, npp, inv):
    nb, _, d = x.shape
    ff = w1.shape[-1]
    nf = nb * T // TF
    dma = pltpu.SemaphoreType.DMA
    act = jax.ShapeDtypeStruct((2, ndp, nb, T, d), BF)
    wide = jax.ShapeDtypeStruct((2, ndp, nb, T, ff), BF)
    flops = 28 * nb * T * d * ff
    return pl.pallas_call(
        functools.partial(_stage_kernel, ndp, npp, nb, inv),
        out_shape=(act, act, wide, wide, jax.ShapeDtypeStruct((ndp, 8, 128), F32)),
        in_specs=[ANY] * 4,
        out_specs=(ANY,) * 5,
        scratch_shapes=[
            pltpu.VMEM((2, d, ff), BF), pltpu.VMEM((2, ff, d), BF),
            pltpu.VMEM((ndp, nb, T, d), BF), pltpu.VMEM((ndp, nb, T, d), BF),
            pltpu.VMEM((2, T, ff), BF), pltpu.VMEM((2, T, ff), BF), pltpu.VMEM((2, T, ff), BF), pltpu.VMEM((2, T, ff), BF),
            pltpu.VMEM((T, d), BF), pltpu.VMEM((T, d), BF), pltpu.VMEM((2, TF, d), BF), pltpu.VMEM((2, T, d), BF),
            pltpu.VMEM((8, 128), F32),
            dma((2, 2)), dma((nf,)), dma((nb,)), dma((nf,)), dma((nb,)), dma((nf,)), dma((nb,)), dma, dma, dma((2,)), dma,
            dma((2, 2)), dma((2, 2)), dma((2,)), dma((2,)), dma((2,)), dma((2,)), dma((ndp * npp,)), dma((ndp,)),
        ],
        compiler_params=pltpu.CompilerParams(collective_id=0, has_side_effects=True, vmem_limit_bytes=67_043_328),
        cost_estimate=pl.CostEstimate(flops=flops, bytes_accessed=16 * nb * T * ff, transcendentals=8 * nb * T * ff),
        name="stage",
    )(x, t, w1, w2)


def _half_kernel(z_ref, h_ref, e_ref, o_ref):
    p = _tn(h_ref[...], e_ref[...])
    k = pl.program_id(0)

    @pl.when(k == 0)
    def _():
        o_ref[...] = p

    @pl.when(k > 0)
    def _():
        o_ref[...] += p


def _half(h, e, z):
    _, n, d = h.shape
    ff = e.shape[-1]
    step = 2048
    return pl.pallas_call(
        _half_kernel,
        grid_spec=pltpu.PrefetchScalarGridSpec(
            num_scalar_prefetch=1,
            grid=(n // step,),
            in_specs=[pl.BlockSpec((None, step, d), lambda k, z: (0, k, 0)),
                      pl.BlockSpec((None, step, ff // 2), lambda k, z: (0, k, z[0]))],
            out_specs=pl.BlockSpec((d, ff // 2), lambda k, z: (0, 0)),
        ),
        out_shape=jax.ShapeDtypeStruct((d, ff // 2), F32),
        compiler_params=pltpu.CompilerParams(vmem_limit_bytes=62 * 1024 * 1024),
        cost_estimate=pl.CostEstimate(flops=n * d * ff, bytes_accessed=n * (2 * d + ff), transcendentals=0),
        name="half",
    )(z, h, e)


def _dw_kernel(h_ref, e_ref, a_ref, g_ref, s_ref, o1_ref, o2_ref, res, tile, o1, o2, sv, rsem, tsem, osem, ssem, vsem):
    z = lax.axis_index("dp")
    ff = e_ref.shape[-1]
    w = tile.shape[-1]
    per = ff // w
    steps = 3 * per
    cols = lambda t: pl.ds(pl.multiple_of(t * w, w), w)

    def resident(p):
        slot = p % 2
        src = h_ref.at[1] if p == 0 else g_ref.at[p - 1]
        return pltpu.make_async_copy(src, res.at[slot], rsem.at[slot])

    def stream_e(i):
        return pltpu.make_async_copy(e_ref.at[1, :, cols(i)], tile.at[lax.rem(i, 2)], tsem.at[lax.rem(i, 2)])

    def stream_a(i):
        j = lax.div(i, per) - 1
        return pltpu.make_async_copy(a_ref.at[j, :, cols(i - per * (j + 1))], tile.at[lax.rem(i, 2)], tsem.at[lax.rem(i, 2)])

    def put1(i):
        return pltpu.make_async_copy(o1.at[lax.rem(i, 2)], o1_ref.at[1, :, cols(i)], osem.at[lax.rem(i, 2)])

    def put2(i):
        j = lax.div(i, per) - 1
        return pltpu.make_async_copy(o2.at[lax.rem(i, 2)], o2_ref.at[j, cols(i - per * (j + 1)), :], osem.at[lax.rem(i, 2)])

    halves = [(pltpu.make_async_copy(s_ref.at[:, pl.ds(t * w, w)], sv.at[t], ssem.at[t]),
               pltpu.make_async_copy(sv.at[t], o1_ref.at[0, :, cols(z * (per // 2) + t)], vsem.at[t])) for t in range(per // 2)]

    resident(0).start()
    stream_e(0).start()

    def step(i, carry):
        @pl.when(i + 1 < per)
        def _():
            stream_e(i + 1).start()

        @pl.when(jnp.logical_and(i + 1 >= per, i + 1 < steps))
        def _():
            stream_a(i + 1).start()

        for p in range(3):
            @pl.when(i == per * p)
            def _():
                resident(p).wait()

            if p < 2:
                @pl.when(i == per * p + 1)
                def _():
                    resident(p + 1).start()
        for t, (get, put) in enumerate(halves):
            @pl.when(i == 2 + 2 * t)
            def _():
                get.start()

            @pl.when(i == 3 + 2 * t)
            def _():
                get.wait()
                put.start()
        k = lax.rem(i, 2)
        pltpu.make_async_copy(e_ref.at[1, :, pl.ds(0, w)], tile.at[k], tsem.at[k]).wait()

        @pl.when(i > 1)
        def _():
            pltpu.make_async_copy(o1.at[k], o1_ref.at[1, :, pl.ds(0, w)], osem.at[k]).wait()
        r = lax.rem(lax.div(i, per), 2)

        @pl.when(i < per)
        def _():
            o1[k] = _tn(res[r], tile[k])
            put1(i).start()

        @pl.when(i >= per)
        def _():
            o2[k] = _tn(tile[k], res[r])
            put2(i).start()
        return carry

    lax.fori_loop(0, steps, step, 0)
    for i in (steps - 2, steps - 1):
        put2(jnp.int32(i)).wait()
    for _, put in halves:
        put.wait()


def _dw(h, e, a, g, half):
    n, d = h.shape[1:]
    ff = e.shape[-1]
    w = 512
    dma = pltpu.SemaphoreType.DMA
    return pl.pallas_call(
        _dw_kernel,
        out_shape=(jax.ShapeDtypeStruct((2, d, ff), F32), jax.ShapeDtypeStruct((2, ff, d), F32)),
        in_specs=[ANY] * 5,
        out_specs=(ANY, ANY),
        scratch_shapes=[
            pltpu.VMEM((2, n, d), BF), pltpu.VMEM((2, n, w), BF), pltpu.VMEM((2, d, w), F32), pltpu.VMEM((2, w, d), F32),
            pltpu.VMEM((ff // w // 2, d, w), F32),
            dma((2,)), dma((2,)), dma((2,)), dma((ff // w // 2,)), dma((ff // w // 2,)),
        ],
        compiler_params=pltpu.CompilerParams(vmem_limit_bytes=62 * 1024 * 1024),
        cost_estimate=pl.CostEstimate(flops=6 * n * d * ff, bytes_accessed=6 * n * ff, transcendentals=0),
        name="dw",
    )(h, e, a, g, half)


def solution(mesh):
    ndp = mesh.shape["dp"]
    npp = mesh.shape["pp"]

    def body(x, t, w1, w2):
        nm, tok, d = x.shape
        ff = w1.shape[-1]
        inv = 1.0 / (nm * tok * ndp * d)
        nb = nm * tok // T
        h, g, a, e, loss = _stages(x.reshape(nb, T, d), t.reshape(nb, T, d), w1[0], w2[0], ndp, npp, inv)
        n = ndp * nb * T
        h, g, a, e = (v.reshape(2, n, v.shape[-1]) for v in (h, g, a, e))
        z = lax.axis_index("dp")
        half = _half(h, e, jnp.full((1,), z, jnp.int32))
        other = lax.ppermute(half, "dp", [(i, (i + 1) % ndp) for i in range(ndp)])
        dw1, dw2 = _dw(h, e, a, g, half)
        dw1 = lax.dynamic_update_slice(dw1, other[None], (0, 0, (1 - z) * (ff // 2)))
        return dw1[None], dw2[None], 0.5 * inv * jnp.sum(loss)

    return jax.shard_map(body, mesh=mesh,
                         in_specs=(P(None, 'dp', None), P(None, 'dp', None), P('pp'), P('pp')),
                         out_specs=(P('pp'), P('pp'), P()), check_vma=False)
```

time: 613 us -> 579 us (0.945); the launches traced: 613 us -> 569 us
  Pallas kernels: 609 us -> 558 us
    pallas_call x1, Pallas kernels: 430 us -> 400 us  [_stages(): pl.pallas_call(functools.partial(_stage_kernel, ndp, npp, nb, inv), out_s...]
    pallas_call x2, Pallas kernels: 179 us -> 157 us  [the longest x1 129 us: _dw(): pl.pallas_call(_dw_kernel, out_shape=(jax.ShapeDtypeStruct((2, d, ff), F3...]
  transfers between devices with their start and end apart: 0 -> 1, of which waited for: 0 -> 0; matrix products, arithmetic and copies ran while one was open for 0% -> 0% of each run, Pallas kernels for 0% -> 23%
where the time goes in v2:
time: 579 us; the launch traced here: 569 us
  Pallas kernels  558 us (96%)
    pallas_call x1, Pallas kernels, _stages(): pl.pallas_call(functools.partial(_stage_kernel, ndp, npp, nb, inv), out_s...  400 us
    pallas_call x1, Pallas kernels, _dw(): pl.pallas_call(_dw_kernel, out_shape=(jax.ShapeDtypeStruct((2, d, ff), F3...  129 us
    pallas_call x1, Pallas kernels, _half(): pl.pallas_call(_half_kernel, grid_spec=pltpu.PrefetchScalarGridSpec(num_s...  27.8 us
  transfers between devices with their start and end apart: 1, of which 0 were waited for; matrix products, arithmetic and copies ran while one was open for 0% of the time, Pallas kernels for 23%

profile of v2, /device:TPU:0, one launch (start us, length us, event | category | flops | bytes accessed | tf_op | source)
XLA Modules:
  0.0 568.9 jit_solution(9118217693290841782)
XLA Ops:
  0.6 400.5 %stage.1 = (bf16[2,2,16,256,768]{4,3,2,1,0:T(8,128)(2,1)}, bf16[2,2,16,256,768]{4,3,2,1,0:T(8,128)(2,1)}, bf16[2,2,16,256,3072]{4,3,2,1,0:T(8,128)(2,1)}, bf16[2...) custom-call(bf16[16,256,768]{2,1,0:T(8,128)(2,1)} %bitcast.18, bf16[16,256,768]{2,1,0:T(8,128)(2,1)} %bitcast.19, ...), custom_call_target="tpu_custom_call" | custom-call | flops 270582939648 | bytes 201326592 | tf_op jit(solution)/shard_map/stage/pallas_call | solution.py:384
  401.1 27.8 %half.1.s_ref = f32[768,1536]{1,0:T(8,128)} custom-call(s32[1]{0:T(128)} %bitcast.8.z_ref, bf16[2,8192,768]{2,1,0:T(8,128)(2,1)} %bitcast.13, bf16[2,8192,3072]{2,1,0:T(8,128)(2,1)} %bitcast.5.e_ref), custom_call_target="tpu_custom_call" | custom-call | flops 19327352832 | bytes 37748736 | tf_op jit(solution)/shard_map/half/pallas_call | solution.py:421
  429.0 3.4 collective-permute-start
  432.4 0.0 copy-start
  432.4 129.2 %dw.1 = (f32[2,768,3072]{2,1,0:T(8,128)}, f32[2,3072,768]{2,1,0:T(8,128)}) custom-call(bf16[2,8192,768]{2,1,0:T(8,128)(2,1)} %bitcast.14, bf16[2,8192,3072]{2,1,0:T(8,128)(2,1)} %bitcast.5.e_ref, bf16[2,8192,3072]{2,1,0:T(8,128)(2,1)} %bitcast.6.a_ref, bf16[2,8192,768]{2,1,0:T(8,128)(2,1)} %bitcast.20, f32[768,1536]{1,0:T(8,128)} %half.1.s_ref), custom_call_target="tpu_custom_call" | custom-call | flops 115964116992 | bytes 150994944 | tf_op jit(solution)/shard_map/dw/pallas_call | solution.py:528
  561.7 0.0 copy-done
  561.7 0.6 reduce_sum.9
  562.9 0.0 collective-permute-done
  562.9 4.9 bitcast_dynamic-update-slice_fusion
Async XLA Ops:
  429.0 134.0 %collective-permute-start = (f32[768,1536]{1,0:T(8,128)}, f32[768,1536]{1,0:T(8,128)}, u32[]{:S(2)}, u32[]{:S(2)}) collective-permute-start(f32[768,1536]{1,0:T(8,128)} %half.1.s_ref), channel_id=1, source_target_pairs={{0,8},{8,0},{1,9},{9,1},{2,10},{10,2},{3,11},{11,3},{4,12},{12,4},... | collective-permute-start | bytes 14155784 | tf_op jit(solution)/shard_map/ppermute | solution.py:558
  432.4 129.3 %copy-start = (f32[2,8,128]{2,1,0:T(8,128)S(1)}, f32[2,8,128]{2,1,0:T(8,128)}, u32[]{:S(2)}) copy-start(f32[2,8,128]{2,1,0:T(8,128)} %get-tuple-element.16) | copy-start | bytes 24580
